TPU v7x, 32 devices: a whole 2x2x4 slice. The times are simulated.
32 devices in a mesh: wide: 16 (over z, y, x), narrow: 2 (over core).
Axes of the slice: x: 2, y: 2, z: 4, core: 2. Of those that a mesh axis runs over, the one named last changes fastest.
Arguments:
- tokens: bfloat16 [32, 200, 768], P(('wide', 'narrow')), may hold values from -6 to 6
- memory_raw: bfloat16 [32, 896, 768], P(('wide', 'narrow')), may hold values from -22 to 22
- lengths: int32 [32], P(('wide', 'narrow')), may hold values from 5 to 200, as said below
- cotangent: bfloat16 [32, 200, 768], P(('wide', 'narrow')), may hold values from -6 to 6
- self_proj: bfloat16 [4, 768, 768], P(None, ('wide', 'narrow')), may hold values from -0.21875 to 0.21875
- cross_proj: bfloat16 [4, 768, 768], P(None, ('wide', 'narrow')), may hold values from -0.21875 to 0.21875
- ffn_pair: bfloat16 [2, 768, 3072], P(None, ('wide', 'narrow')), may hold values from -0.21875 to 0.21875
- ffn_gain: bfloat16 [3072], P(('wide', 'narrow')), may hold values from 0.5 to 1.5
- norm_gains: bfloat16 [5, 768], P(None, ('wide', 'narrow')), may hold values from 0.5 to 1.5
- rel_table: bfloat16 [512, 12], P(('wide', 'narrow')), may hold values from -5 to 5
- head_gain: bfloat16 [2, 12], replicated, may hold values from 0.099609375 to 1.8984375
- bn_scale: bfloat16 [768], P(('wide', 'narrow')), may hold values from 0.099609375 to 1.8984375
- bn_bias: bfloat16 [768], P(('wide', 'narrow')), may hold values from -3 to 3
Outputs:
- output: bfloat16 [32, 200, 768], P(('wide', 'narrow'))
- d_tokens: float32 [32, 200, 768], P(('wide', 'narrow'))
- d_memory: float32 [32, 896, 768], P(('wide', 'narrow'))
- d_self_proj: float32 [4, 768, 768], P(None, ('wide', 'narrow'))
- d_cross_proj: float32 [4, 768, 768], P(None, ('wide', 'narrow'))
- d_ffn_pair: float32 [2, 768, 3072], P(None, ('wide', 'narrow'))
- d_ffn_gain: float32 [3072], P(('wide', 'narrow'))
- d_norm_gains: float32 [5, 768], P(None, ('wide', 'narrow'))
- d_rel_table: float32 [512, 12], P(('wide', 'narrow'))
- d_head_gain: float32 [2, 12], replicated
- d_bn_scale: float32 [768], P(('wide', 'narrow'))
- d_bn_bias: float32 [768], P(('wide', 'narrow'))
Inputs may be any that keep to these rules, and one draw needn't show every extreme that they name: `lengths`: some item has exactly 200 decoder tokens in every draw.
All inputs are finite; a program needn't handle non-finite values.
Results may differ from a plain program's by a relative error of at most 0.02.
Values may be sent and summed in bfloat16 or wider, within the bound.
A program may use at most 256 MiB of HBM per device.

v0:
```python
from functools import partial
import math
import jax
import jax.numpy as jnp
import numpy as np
from jax import lax
from jax.sharding import PartitionSpec as P

EPSILON = 1e-05
NEGATIVE = -1000000000.0
HIGHEST = lax.Precision.HIGHEST


def bucket_select(length, buckets):
    select = np.zeros((buckets, length), np.float32)
    for distance in range(length):
        if distance <= 128:
            bucket = 255 - distance
        else:
            scaled = math.log(distance / 128.0) / math.log(1023.0 / 128.0) * 127.0
            bucket = 255 - (int(math.ceil(scaled)) + 128)
        select[bucket, distance] = 1.0
    return select


def toeplitz(by_distance):
    head_count, row_count = by_distance.shape
    padded = jnp.concatenate([by_distance[:, ::-1], jnp.zeros_like(by_distance)], axis=1)
    repeated = jnp.tile(padded, (1, row_count))[:, : row_count * (2 * row_count - 1)]
    shaped = repeated.reshape(head_count, row_count, 2 * row_count - 1)
    return shaped[:, :, row_count - 1 :]


def norm_forward(values, gain_row):
    centred = values - jnp.mean(values, axis=-1, keepdims=True)
    variance = jnp.mean(centred * centred, axis=-1, keepdims=True)
    return centred * lax.rsqrt(variance + EPSILON) * gain_row


def norm_backward(values, gain_row, upstream):
    unused, pullback = jax.vjp(norm_forward, values, gain_row)
    return pullback(upstream)


def product(left_side, right_side):
    return jnp.dot(left_side, right_side, preferred_element_type=jnp.float32)


def back_product(upstream, weight):
    return jnp.einsum("ble,de->bld", upstream, weight, preferred_element_type=jnp.float32)


def weight_grad(activation, upstream):
    return jnp.einsum("bld,ble->de", activation, upstream, preferred_element_type=jnp.float32)


def to_heads(values, head_count):
    return values.reshape(
        values.shape[0], values.shape[1], head_count, values.shape[2] // head_count
    )


def from_heads(values):
    return values.reshape(values.shape[0], values.shape[1], values.shape[2] * values.shape[3])


def attend_scores(queries, key_rows, score_bias, allowed, inv_root):
    scores = (
        jnp.einsum("bqhe,bkhe->bhqk", queries, key_rows, preferred_element_type=jnp.float32)
        * inv_root
    )
    if score_bias is None:
        return scores
    return jnp.where(allowed, scores + score_bias, NEGATIVE)


def attend_forward(queries, key_rows, values, score_bias, allowed, head_scale, inv_root):
    scores = attend_scores(queries, key_rows, score_bias, allowed, inv_root)
    maximum = jnp.max(scores, axis=-1, keepdims=True)
    totals = maximum + jnp.log(jnp.sum(jnp.exp(scores - maximum), axis=-1, keepdims=True))
    softmax_low = jnp.exp(scores - totals).astype(jnp.bfloat16)
    attended = jnp.einsum(
        "bhqk,bkhe->bqhe", softmax_low, values, preferred_element_type=jnp.float32
    )
    scaled = (attended * head_scale[:, None]).astype(jnp.bfloat16)
    return (attended, from_heads(scaled), totals)


def attend_backward(
    queries, key_rows, values, score_bias, allowed, head_scale, inv_root, totals, attended, upstream
):
    head_grad = jnp.sum(upstream * attended, axis=(0, 1, 3))
    grad_attended = (upstream * head_scale[:, None]).astype(jnp.bfloat16)
    softmax_out = jnp.exp(attend_scores(queries, key_rows, score_bias, allowed, inv_root) - totals)
    softmax_low = softmax_out.astype(jnp.bfloat16)
    grad_soft = jnp.einsum(
        "bqhe,bkhe->bhqk", grad_attended, values, preferred_element_type=jnp.float32
    )
    grad_values = jnp.einsum(
        "bhqk,bqhe->bkhe", softmax_low, grad_attended, preferred_element_type=jnp.float32
    )
    grad_scores = softmax_out * (
        grad_soft - jnp.sum(softmax_out * grad_soft, axis=-1, keepdims=True)
    )
    grad_scores = grad_scores.astype(jnp.bfloat16)
    grad_queries = (
        jnp.einsum("bhqk,bkhe->bqhe", grad_scores, key_rows, preferred_element_type=jnp.float32)
        * inv_root
    )
    grad_keys = (
        jnp.einsum("bhqk,bqhe->bkhe", grad_scores, queries, preferred_element_type=jnp.float32)
        * inv_root
    )
    return (
        head_grad,
        grad_scores,
        from_heads(grad_queries.astype(jnp.bfloat16)),
        from_heads(grad_keys.astype(jnp.bfloat16)),
        from_heads(grad_values.astype(jnp.bfloat16)),
    )


def body(
    tokens,
    memory_raw,
    lengths,
    cotangent,
    self_proj,
    cross_proj,
    ffn_pair,
    ffn_gain,
    norm_gains,
    rel_table,
    head_gain,
    bn_scale,
    bn_bias,
):
    item_count, length, model_width = tokens.shape
    head_count = head_gain.shape[1]
    inv_root = 1.0 / math.sqrt(model_width // head_count)
    mem_rows = memory_raw.shape[1]
    head_scales = head_gain.astype(jnp.float32)
    self_full, gains_full, table_full = (
        lax.all_gather(self_proj, ("wide", "narrow"), axis=1, tiled=True),
        lax.all_gather(norm_gains, ("wide", "narrow"), axis=1, tiled=True),
        lax.all_gather(rel_table, ("wide", "narrow"), axis=0, tiled=True),
    )
    norm_scale = gains_full.astype(jnp.float32)
    select = jnp.asarray(bucket_select(length, table_full.shape[0]))
    by_distance = jnp.einsum("th,td->hd", table_full.astype(jnp.float32), select, precision=HIGHEST)
    score_bias = toeplitz(by_distance)[None]
    positions = jnp.arange(length)
    causal = positions[None, :] <= positions[:, None]
    live_keys = positions[None, :] < lengths[:, None]
    allowed = causal[None, None] & live_keys[:, None, None, :]
    token_values = tokens.astype(jnp.float32)
    normed_one = norm_forward(token_values, norm_scale[0]).astype(jnp.bfloat16)
    self_queries = to_heads(product(normed_one, self_full[0]).astype(jnp.bfloat16), head_count)
    self_keys = to_heads(product(normed_one, self_full[1]).astype(jnp.bfloat16), head_count)
    self_values = to_heads(product(normed_one, self_full[2]).astype(jnp.bfloat16), head_count)
    self_attended, self_flat, self_totals = attend_forward(
        self_queries, self_keys, self_values, score_bias, allowed, head_scales[0], inv_root
    )
    self_branch = product(self_flat, self_full[3])
    residual_one = token_values + norm_forward(self_branch, norm_scale[1])
    cross_full, scale_full, shift_full = (
        lax.all_gather(cross_proj, ("wide", "narrow"), axis=1, tiled=True),
        lax.all_gather(bn_scale, ("wide", "narrow"), axis=0, tiled=True),
        lax.all_gather(bn_bias, ("wide", "narrow"), axis=0, tiled=True),
    )
    memory_values = memory_raw.astype(jnp.float32)
    plain_sum, square_sum = lax.psum(
        (jnp.sum(memory_values, axis=(0, 1)), jnp.sum(memory_values * memory_values, axis=(0, 1))),
        ("wide", "narrow"),
    )
    row_total = item_count * mem_rows * lax.axis_size(("wide", "narrow"))
    bn_mean = plain_sum / row_total
    inv_std = lax.rsqrt(square_sum / row_total - bn_mean * bn_mean + EPSILON)
    centred_mem = (memory_values - bn_mean) * inv_std
    bn_gain = scale_full.astype(jnp.float32)
    memory_low = (centred_mem * bn_gain + shift_full.astype(jnp.float32)).astype(jnp.bfloat16)
    normed_two = norm_forward(residual_one, norm_scale[2]).astype(jnp.bfloat16)
    cross_queries = to_heads(product(normed_two, cross_full[0]).astype(jnp.bfloat16), head_count)
    cross_keys = to_heads(product(memory_low, cross_full[1]).astype(jnp.bfloat16), head_count)
    cross_values = to_heads(product(memory_low, cross_full[2]).astype(jnp.bfloat16), head_count)
    cross_attended, cross_flat, cross_totals = attend_forward(
        cross_queries, cross_keys, cross_values, None, None, head_scales[1], inv_root
    )
    cross_branch = product(cross_flat, cross_full[3])
    residual_two = residual_one + norm_forward(cross_branch, norm_scale[3])
    ffn_full, ffn_scale = (
        lax.all_gather(ffn_pair, ("wide", "narrow"), axis=1, tiled=True),
        lax.all_gather(ffn_gain, ("wide", "narrow"), axis=0, tiled=True),
    )
    normed_three = norm_forward(residual_two, norm_scale[4]).astype(jnp.bfloat16)
    hidden = product(normed_three, ffn_full[0])
    activated = jax.nn.gelu(hidden, approximate=False)
    unit_scale = ffn_scale.astype(jnp.float32)
    rescaled = norm_forward(activated, unit_scale).astype(jnp.bfloat16)
    ffn_branch = jnp.einsum(
        "blf,df->bld", rescaled, ffn_full[1], preferred_element_type=jnp.float32
    )
    output = (residual_two + ffn_branch).astype(jnp.bfloat16)
    ffn_back = lax.all_gather(ffn_pair, ("wide", "narrow"), axis=1, tiled=True)
    upstream = cotangent.astype(jnp.float32)
    grad_rescaled = jnp.einsum(
        "bld,df->blf", cotangent, ffn_back[1], preferred_element_type=jnp.float32
    )
    grad_activated, grad_unit_scale = norm_backward(activated, unit_scale, grad_rescaled)
    unused, gelu_pull = jax.vjp(partial(jax.nn.gelu, approximate=False), hidden)
    grad_hidden = gelu_pull(grad_activated)[0].astype(jnp.bfloat16)
    grad_normed_three = jnp.einsum(
        "blf,df->bld", grad_hidden, ffn_back[0], preferred_element_type=jnp.float32
    )
    grad_two_part, grad_scale_four = norm_backward(residual_two, norm_scale[4], grad_normed_three)
    grad_res_two = upstream + grad_two_part
    grad_in = weight_grad(normed_three, grad_hidden)
    grad_out = weight_grad(cotangent, rescaled)
    ffn_grad_shard = jnp.transpose(
        lax.psum_scatter(
            jnp.stack([grad_in, grad_out], axis=1),
            ("wide", "narrow"),
            scatter_dimension=0,
            tiled=True,
        ),
        (1, 0, 2),
    )
    cross_back = lax.all_gather(cross_proj, ("wide", "narrow"), axis=1, tiled=True)
    grad_cross_branch, grad_scale_three = norm_backward(cross_branch, norm_scale[3], grad_res_two)
    grad_cross_low = grad_cross_branch.astype(jnp.bfloat16)
    grad_cross_scaled = to_heads(back_product(grad_cross_low, cross_back[3]), head_count)
    cross_head, unused_scores, grad_cross_query, grad_cross_key, grad_cross_value = attend_backward(
        cross_queries,
        cross_keys,
        cross_values,
        None,
        None,
        head_scales[1],
        inv_root,
        cross_totals,
        cross_attended,
        grad_cross_scaled,
    )
    grad_memory = back_product(grad_cross_key, cross_back[1]) + back_product(
        grad_cross_value, cross_back[2]
    )
    grad_one_part, grad_scale_two = norm_backward(
        residual_one, norm_scale[2], back_product(grad_cross_query, cross_back[0])
    )
    grad_res_one = grad_res_two + grad_one_part
    cross_grad_shard = jnp.transpose(
        lax.psum_scatter(
            jnp.stack(
                [
                    weight_grad(normed_two, grad_cross_query),
                    weight_grad(memory_low, grad_cross_key),
                    weight_grad(memory_low, grad_cross_value),
                    weight_grad(cross_flat, grad_cross_low),
                ],
                axis=1,
            ),
            ("wide", "narrow"),
            scatter_dimension=0,
            tiled=True,
        ),
        (1, 0, 2),
    )
    self_back = lax.all_gather(self_proj, ("wide", "narrow"), axis=1, tiled=True)
    grad_self_branch, grad_scale_one = norm_backward(self_branch, norm_scale[1], grad_res_one)
    grad_self_low = grad_self_branch.astype(jnp.bfloat16)
    grad_self_scaled = to_heads(back_product(grad_self_low, self_back[3]), head_count)
    self_head, grad_bias_scores, grad_self_query, grad_self_key, grad_self_value = attend_backward(
        self_queries,
        self_keys,
        self_values,
        score_bias,
        allowed,
        head_scales[0],
        inv_root,
        self_totals,
        self_attended,
        grad_self_scaled,
    )
    grad_bias = jnp.sum(grad_bias_scores.astype(jnp.float32), axis=0)
    unused_value, toeplitz_pull = jax.vjp(toeplitz, by_distance)
    grad_distance = toeplitz_pull(grad_bias)[0]
    grad_table = jnp.einsum("td,hd->th", select, grad_distance, precision=HIGHEST)
    grad_normed_one = (
        back_product(grad_self_query, self_back[0])
        + back_product(grad_self_key, self_back[1])
        + back_product(grad_self_value, self_back[2])
    )
    grad_tokens_part, grad_scale_zero = norm_backward(token_values, norm_scale[0], grad_normed_one)
    grad_tokens = grad_res_one + grad_tokens_part
    gain_grads = jnp.stack(
        [grad_scale_zero, grad_scale_one, grad_scale_two, grad_scale_three, grad_scale_four]
    )
    self_grad_shard = jnp.transpose(
        lax.psum_scatter(
            jnp.stack(
                [
                    weight_grad(normed_one, grad_self_query),
                    weight_grad(normed_one, grad_self_key),
                    weight_grad(normed_one, grad_self_value),
                    weight_grad(self_flat, grad_self_low),
                ],
                axis=1,
            ),
            ("wide", "narrow"),
            scatter_dimension=0,
            tiled=True,
        ),
        (1, 0, 2),
    )
    bias_part = jnp.sum(grad_memory, axis=(0, 1))
    scale_part = jnp.sum(grad_memory * centred_mem, axis=(0, 1))
    bn_totals, head_totals, gain_totals, table_totals, unit_totals = lax.psum(
        (
            jnp.stack([scale_part, bias_part]),
            jnp.stack([self_head, cross_head]),
            gain_grads,
            grad_table,
            grad_unit_scale,
        ),
        ("wide", "narrow"),
    )
    grad_memory_raw = (
        bn_gain
        * inv_std
        * (grad_memory - bn_totals[1] / row_total - centred_mem * (bn_totals[0] / row_total))
    )
    position = lax.axis_index(("wide", "narrow"))
    shard_width = bn_scale.shape[0]
    offset = position * shard_width
    bn_scale_shard = lax.dynamic_slice_in_dim(bn_totals[0], offset, shard_width)
    bn_bias_shard = lax.dynamic_slice_in_dim(bn_totals[1], offset, shard_width)
    gain_shard = lax.dynamic_slice_in_dim(gain_totals, offset, shard_width, 1)
    table_rows = rel_table.shape[0]
    table_shard = lax.dynamic_slice_in_dim(table_totals, position * table_rows, table_rows, 0)
    unit_width = ffn_gain.shape[0]
    ffn_gain_shard = lax.dynamic_slice_in_dim(unit_totals, position * unit_width, unit_width)
    return (
        output,
        grad_tokens,
        grad_memory_raw,
        self_grad_shard,
        cross_grad_shard,
        ffn_grad_shard,
        ffn_gain_shard,
        gain_shard,
        table_shard,
        head_totals,
        bn_scale_shard,
        bn_bias_shard,
    )


def solution(mesh):
    return jax.shard_map(
        body,
        mesh=mesh,
        in_specs=(
            P(("wide", "narrow"), None, None),
            P(("wide", "narrow"), None, None),
            P(("wide", "narrow")),
            P(("wide", "narrow"), None, None),
            P(None, ("wide", "narrow"), None),
            P(None, ("wide", "narrow"), None),
            P(None, ("wide", "narrow"), None),
            P(("wide", "narrow")),
            P(None, ("wide", "narrow")),
            P(("wide", "narrow"), None),
            P(),
            P(("wide", "narrow")),
            P(("wide", "narrow")),
        ),
        out_specs=(
            P(("wide", "narrow"), None, None),
            P(("wide", "narrow"), None, None),
            P(("wide", "narrow"), None, None),
            P(None, ("wide", "narrow"), None),
            P(None, ("wide", "narrow"), None),
            P(None, ("wide", "narrow"), None),
            P(("wide", "narrow")),
            P(None, ("wide", "narrow")),
            P(("wide", "narrow"), None),
            P(),
            P(("wide", "narrow")),
            P(("wide", "narrow")),
        ),
        check_vma=False,
    )
```

profile of v0, /device:TPU:0, one launch (start us, length us, event | category | flops | bytes accessed | tf_op | source)
XLA Modules:
  0.0 789.1 jit_solution(18137950825026918576)
XLA Ops:
  13.3 42.3 %all-reduce.8 = (bf16[768]{0:T(1024)(128)(2,1)S(1)}, bf16[768]{0:T(1024)(128)(2,1)S(1)}, bf16[3072]{0:T(1024)(128)(2,1)S(1)}) all-reduce(bf16[768]{0:T(1024)(128)(2,1)S(1)} %dynamic-update-slice.1, bf16[768]{0:T(1024)(128)(2,1)S(1)} %dynamic-update-slice, ...), channel_id=1, replica_groups=mesh['wide'=16,'narrow'=2] {'wide','narrow'}, use_global_device_ids=true, to_apply=%add.4 | all-reduce | flops 4608 | bytes 18432
  57.4 40.9 %all-gather = bf16[32,24,5]{1,2,0:T(8,128)(2,1)S(1)} all-gather(bf16[1,24,5]{1,2,0:T(8,128)(2,1)} %bitcast.348), channel_id=1, replica_groups=mesh['wide'=16,'narrow'=2] {'wide','narrow'}, dimensions={0}, use_global_device_ids=true | all-gather | bytes 7920 | tf_op jit(solution)/shard_map/all_gather | solution.py:145
  98.6 37.8 %all_gather.29 = bf16[512,12]{1,0:T(8,128)(2,1)S(1)} all-gather(bf16[16,12]{1,0:T(8,128)(2,1)} %param.23), channel_id=1, replica_groups=mesh['wide'=16,'narrow'=2] {'wide','narrow'}, dimensions={0}, use_global_device_ids=true | all-gather | bytes 12672 | tf_op jit(solution)/shard_map/all_gather | solution.py:146
  138.0 2.9 tile.4
  140.9 7.0 tile.10
  147.9 5.1 slice.107
  153.0 7.2 reshape.913
  160.2 4.2 slice.108
  164.4 3.4 copy.99
  168.2 39.5 %all-reduce.7 = (f32[768]{0:T(1024)S(1)}, f32[768]{0:T(1024)S(1)}) all-reduce(f32[768]{0:T(1024)S(1)} %get-tuple-element.19, f32[768]{0:T(1024)S(1)} %get-tuple-element.18), channel_id=1, replica_groups=mesh['wide'=16,'narrow'=2] {'wide','narrow'}, use_global_device_ids=true, to_apply=%region_9.10 | all-reduce | flops 1536 | bytes 12288 | tf_op jit(solution)/shard_map/psum | solution.py:172
  210.6 1.8 convolution_convert_fusion.6
  212.6 1.9 convolution_convert_fusion.5
  215.4 1.8 convolution_convert_fusion.7
  217.3 2.6 fusion.107
  220.6 1.4 multiply_convert_fusion.7
  222.0 2.0 fusion.108
  225.5 2.6 convolution_convert_fusion.4
  228.1 1.9 copy.82
  230.0 3.3 convolution_convert_fusion.1
  233.4 1.6 multiply_reduce_fusion.1
  235.0 1.8 exponential_reduce_fusion
  237.3 1.5 convolution_convert_fusion.2
  238.9 3.2 multiply_convert_fusion.6
  244.9 8.3 %fusion.103 = (f32[200]{0:T(256)S(1)}, f32[200,3072]{1,0:T(8,128)S(1)}, f32[200,3072]{1,0:T(8,128)S(1)}, f32[200,3072]{1,0:T(8,128)S(1)}) fusion(bf16[2,768,3072]{2,1,0:T(8,128)(2,1)} %all-gather.9.cloned.1.call-done, f32[1,200,768]{2,1,0:T(8,128)} %copy-done.20, f32[768]{0:T(1024)S(1)} %copy-done.63, f32[200]{0:T(256)S(1)} %fusion.72, ...), kind=kOutput, calls=%fused_computation.231 | convolution fusion | flops 984268608 | bytes 12711264 | tf_op jit(solution)/shard_map/dot_general | solution.py:46
  253.3 1.5 multiply_reduce_fusion.4
  254.8 1.6 multiply_reduce_fusion.2
  256.4 2.0 add_convert_fusion
  258.4 2.4 fusion.49
  262.6 2.1 fusion.35
  264.8 4.1 multiply_reduce_fusion
  268.9 2.1 multiply_convert_fusion
  271.0 1.6 fusion.24
  273.0 2.7 fusion.51
  277.5 1.8 fusion.31
  286.3 3.9 pad_maximum_fusion.1
  293.0 3.4 multiply_convert_fusion.1
  296.4 6.2 convolution_convert_fusion
  302.7 1.6 convolution_bitcast_fusion.3
  304.3 1.6 convolution_bitcast_fusion.4
  305.9 4.0 pad_maximum_fusion.2
  310.2 3.3 convolution_bitcast_fusion.1
  313.6 1.6 convolution_bitcast_fusion
  315.1 7.3 pad_maximum_fusion
  322.5 2.5 copy.100
  330.1 2.1 fusion.30
  332.2 1.9 convolution_add_fusion.2
  334.2 2.1 fusion.48
  338.6 2.2 pad.9.clone
  340.8 6.7 reshape.933
  347.6 3.1 fusion.34
  350.7 2.7 fusion.110
  356.2 2.6 pad_convert_fusion
  358.7 7.9 reshape.939
  366.6 3.7 reduce_sum.426
  371.7 1.4 reverse.1
  373.1 1.3 stack.96
  374.5 1.4 multiply_reduce_fusion.6
  375.9 1.6 multiply_reduce_fusion.7
  378.9 48.3 %all-reduce.6 = (f32[2,768]{1,0:T(2,128)S(1)}, f32[3072]{0:T(1024)S(1)}, f32[5,768]{1,0:T(8,128)S(1)}, f32[512,12]{1,0:T(8,128)}, f32[2,12]{1,0:T(2,128)}) all-reduce(f32[2,768]{1,0:T(2,128)S(1)} %pad_maximum_fusion.3, f32[3072]{0:T(1024)} %get-tuple-element.12, ...), channel_id=1, replica_groups=mesh['wide'=16,'narrow'=2] {'wide','narrow'}, use_global_device_ids=true, to_apply=%region_36.37 | all-reduce | flops 14616 | bytes 116928 | tf_op jit(solution)/shard_map/psum | solution.py:317
  430.5 2.2 add_add_fusion.6
  432.7 4.0 fusion.13
  436.7 4.9 fusion.29
  441.6 129.6 %reduce-scatter.6.cloned.1.call-done = f32[24,4,768]{2,0,1:T(8,128)} async-done(((f32[768,4,768]{2,0,1:T(8,128)}), f32[24,4,768]{2,0,1:T(8,128)}) %reduce-scatter.6.cloned.1.call-update) | async-done | bytes 294928 | tf_op jit(solution)/shard_map/reduce_scatter | solution.py:252
  571.1 210.9 %reduce-scatter.8.cloned.1.call-done = f32[24,2,3072]{2,0,1:T(8,128)} async-done(((f32[768,2,3072]{2,0,1:T(8,128)}), f32[24,2,3072]{2,0,1:T(8,128)}) %reduce-scatter.8.cloned.1.call-update) | async-done | bytes 589840 | tf_op jit(solution)/shard_map/reduce_scatter | solution.py:220
  (340 shorter events, 48.7 us)
Async XLA Ops:
  7.2 203.4 %all-gather.5.cloned.1.call-start = ((), (), s32[]{:S(2)}) async-start(), calls=%async_computation.3 | async-start | bytes 4866048 | tf_op jit(solution)/shard_map/all_gather | solution.py:144
  7.9 217.5 %all-gather.7.cloned.1.call-start = ((), (), s32[]{:S(2)}) async-start(), calls=%async_computation.4 | async-start | bytes 4866048 | tf_op jit(solution)/shard_map/all_gather | solution.py:167
  8.7 236.2 %all-gather.9.cloned.1.call-start = ((), (), s32[]{:S(2)}) async-start(), calls=%async_computation.5 | async-start | bytes 9732096 | tf_op jit(solution)/shard_map/all_gather | solution.py:192
  9.4 432.2 %reduce-scatter.4.cloned.1.call-start = ((), (), s32[]{:S(2)}) async-start(), calls=%async_computation.6 | async-start | bytes 9732096 | tf_op jit(solution)/shard_map/reduce_scatter | solution.py:299
  164.4 3.4 copy-start.9
  164.4 44.0 %copy-start.4 = (bf16[1,200,768]{2,1,0:T(8,128)(2,1)S(1)}, bf16[1,200,768]{2,1,0:T(8,128)(2,1)}, u32[]{:S(2)}) copy-start(bf16[1,200,768]{2,1,0:T(8,128)(2,1)} %param.14) | copy-start | bytes 921604
  208.5 6.9 copy-start.67
  208.7 5.7 copy-start.95
  209.3 6.1 copy-start.71
  212.5 4.8 copy-start.45
  222.0 3.4 copy-start.75
  224.8 5.1 copy-start.76
  224.8 5.1 copy-start.80
  224.8 5.1 copy-start.102
  224.8 5.1 copy-start.104
  230.0 6.8 slice-start.3
  233.3 3.5 slice-start.4
  235.0 3.9 copy-start
  237.3 31.6 %copy-start.58 = (f32[12,200]{1,0:T(8,128)}, f32[12,200]{1,0:T(8,128)S(1)}, u32[]{:S(2)}) copy-start(f32[12,200]{1,0:T(8,128)S(1)} %log_add_fusion) | copy-start | bytes 28804
  243.8 17.1 %copy-start.84 = (f32[200]{0:T(256)}, f32[200]{0:T(256)S(1)}, u32[]{:S(2)}) copy-start(f32[200]{0:T(256)S(1)} %broadcast_multiply_fusion.2) | copy-start | bytes 2404
  244.8 16.0 %copy-start.91 = (f32[200]{0:T(256)}, f32[200]{0:T(256)S(1)}, u32[]{:S(2)}) copy-start(f32[200]{0:T(256)S(1)} %fusion.72) | copy-start | bytes 2404
  244.8 8.4 %copy-start.33 = (bf16[1,200,768]{2,1,0:T(8,128)(2,1)S(1)}, bf16[1,200,768]{2,1,0:T(8,128)(2,1)}, u32[]{:S(2)}) copy-start(bf16[1,200,768]{2,1,0:T(8,128)(2,1)} %param.17) | copy-start | bytes 921604
  244.9 8.4 %copy-start.60 = (f32[3072]{0:T(1024)S(1)}, f32[3072]{0:T(1024)}, u32[]{:S(2)}) copy-start(f32[3072]{0:T(1024)} %convert_element_type.192) | copy-start | bytes 36868
  244.9 8.4 %copy-start.107 = (bf16[2,768,3072]{2,1,0:T(8,128)(2,1)S(1)}, bf16[2,768,3072]{2,1,0:T(8,128)(2,1)}, u32[]{:S(2)}) copy-start(bf16[2,768,3072]{2,1,0:T(8,128)(2,1)} %all-gather.9.cloned.1.call-done) | copy-start | bytes 28311556
  258.4 6.3 slice-start
  258.4 6.3 slice-start.1
  260.8 3.9 slice-start.2
  262.6 6.2 copy-start.26
  264.7 4.2 copy-start.6
  280.6 3.7 copy-start.40
  290.3 280.9 %reduce-scatter.6.cloned.1.call-start = ((), (), s32[]{:S(2)}) async-start(), calls=%async_computation.7 | async-start | bytes 9732096 | tf_op jit(solution)/shard_map/reduce_scatter | solution.py:252
  293.0 3.4 copy-start.59
  293.0 3.4 copy-start.100
  296.4 8.0 %copy-start.55 = (bf16[12,64,896]{2,1,0:T(8,128)(2,1)}, bf16[12,64,896]{2,1,0:T(8,128)(2,1)S(1)}, u32[]{:S(2)}) copy-start(bf16[12,64,896]{2,1,0:T(8,128)(2,1)S(1)} %multiply_convert_fusion.1) | copy-start | bytes 4128772
  296.4 6.3 copy-start.11
  296.4 6.3 copy-start.77
  296.4 6.3 copy-start.81
  296.4 6.3 copy-start.103
  296.4 6.3 copy-start.105
  309.9 3.6 copy-start.3
  309.9 472.1 %reduce-scatter.8.cloned.1.call-start = ((), (), s32[]{:S(2)}) async-start(), calls=%async_computation.8 | async-start | bytes 19464192 | tf_op jit(solution)/shard_map/reduce_scatter | solution.py:220
  310.1 3.4 copy-start.34
  310.1 3.4 copy-start.61
  310.2 3.4 copy-start.86
  310.2 3.4 copy-start.89
  325.0 7.2 copy-start.43
  330.1 4.0 copy-start.41
  330.1 4.0 copy-start.69
  332.2 4.0 copy-start.96
  332.2 4.8 copy-start.73
  334.1 4.5 copy-start.32
  375.9 54.5 %copy-start.106 = (f32[200]{0:T(256)S(1)}, f32[200]{0:T(256)}, u32[]{:S(2)}) copy-start(f32[200]{0:T(256)} %get-tuple-element.27) | copy-start | bytes 2404
  375.9 54.5 %copy-start.24 = (f32[1,200,768]{2,1,0:T(8,128)S(1)}, f32[1,200,768]{2,1,0:T(8,128)}, u32[]{:S(2)}) copy-start(f32[1,200,768]{2,1,0:T(8,128)} %copy-done.23) | copy-start | bytes 1843204
  375.9 54.5 %copy-start.70 = (f32[200]{0:T(256)S(1)}, f32[200]{0:T(256)}, u32[]{:S(2)}) copy-start(f32[200]{0:T(256)} %copy-done.67) | copy-start | bytes 2404
  375.9 54.5 %copy-start.74 = (f32[200]{0:T(256)S(1)}, f32[200]{0:T(256)}, u32[]{:S(2)}) copy-start(f32[200]{0:T(256)} %copy-done.71) | copy-start | bytes 2404
  375.9 54.5 %copy-start.98 = (f32[200]{0:T(256)S(1)}, f32[200]{0:T(256)}, u32[]{:S(2)}) copy-start(f32[200]{0:T(256)} %copy-done.97) | copy-start | bytes 2404
  375.9 56.7 %copy-start.79 = (f32[768]{0:T(1024)S(1)}, f32[768]{0:T(1024)}, u32[]{:S(2)}) copy-start(f32[768]{0:T(1024)} %get-tuple-element.62) | copy-start | bytes 9220
  375.9 56.7 %copy-start.83 = (f32[768]{0:T(1024)S(1)}, f32[768]{0:T(1024)}, u32[]{:S(2)}) copy-start(f32[768]{0:T(1024)} %get-tuple-element.65) | copy-start | bytes 9220
  375.9 56.7 %copy-start.92 = (f32[768]{0:T(1024)S(1)}, f32[768]{0:T(1024)}, u32[]{:S(2)}) copy-start(f32[768]{0:T(1024)} %get-tuple-element.61) | copy-start | bytes 9220
  427.2 5.4 copy-start.13
  432.6 4.0 copy-start.22
  432.6 4.0 copy-start.62
  432.6 4.0 copy-start.87
  432.7 4.0 copy-start.90
  (55 other events, 119.0 us)
Sparse Core Ops, SparseCore 0:
  10.9 66.7 all-gather.4
  80.7 61.9 all-gather.6
  145.6 81.8 all-gather.8
  290.4 139.1 reduce-scatter.3
  435.9 135.1 reduce-scatter.5
  578.0 203.9 reduce-scatter.7
where the time goes:
time: 798 us; the launch traced here: 789 us
  waiting for transfers between devices  343 us (43%)
  blocking collectives  209 us (26%)
  matrix products  91.6 us (11%)
  local copies, waits for them, and re-layouts  78.9 us (10%)
  other arithmetic  50.1 us (6%)
  between operations  16.6 us (2%)
    reduce_scatter x1, waiting for transfers between devices, body(): lax.psum_scatter(jnp.stack([grad_in, grad_out], axis=1), ('wide', 'narrow...  211 us
    reduce_scatter x1, waiting for transfers between devices, body(): lax.psum_scatter(jnp.stack([weight_grad(normed_two, grad_cross_query), we...  130 us
    psum x1, blocking collectives, body(): lax.psum((jnp.stack([scale_part, bias_part]), jnp.stack([self_head, cross...  48.3 us
    unnamed x1, blocking collectives  42.3 us
    all_gather x1, blocking collectives, body(): lax.all_gather(norm_gains, ('wide', 'narrow'), axis=1, tiled=True)  40.9 us
    psum x1, blocking collectives, body(): lax.psum((jnp.sum(memory_values, axis=(0, 1)), jnp.sum(memory_values * me...  39.5 us
    all_gather x1, blocking collectives, body(): lax.all_gather(rel_table, ('wide', 'narrow'), axis=0, tiled=True)  37.8 us
    dot_general x9, matrix products, product(): return jnp.dot(left_side, right_side, preferred_element_type=jnp.float32)  23.7 us
  transfers between devices with their start and end apart: 6, of which 2 were waited for; matrix products, arithmetic and copies ran while one was open for 21% of the time, Pallas kernels for 0%

commit v1 on v0

--- a/solution.py
+++ b/solution.py
@@ -9,6 +9,28 @@
 EPSILON = 1e-05
 NEGATIVE = -1000000000.0
 HIGHEST = lax.Precision.HIGHEST
+
+
+def in_order(blocks, dim):
+    blocks = jnp.moveaxis(blocks, 0, dim)
+    shape = blocks.shape
+    return blocks.reshape(*shape[:dim], shape[dim] * shape[dim + 1], *shape[dim + 2 :])
+
+
+def collected_by_bits(value, axis):
+    peers = lax.axis_size(axis)
+    blocks = value[None]
+    for level in range(peers.bit_length() - 1):
+        bit = 1 << level
+        other = lax.ppermute(blocks, axis, [(i, i ^ bit) for i in range(peers)])
+        both = jnp.stack([blocks, other])
+        upper = lax.axis_index(axis) >> level & 1
+        blocks = jnp.where(upper == 0, both, both[::-1]).reshape(-1, *value.shape)
+    return blocks
+
+
+def doubled_up(array, axis, dim):
+    return in_order(collected_by_bits(array, axis), dim)
 
 
 def bucket_select(length, buckets):
@@ -143,7 +165,7 @@
     self_full, gains_full, table_full = (
         lax.all_gather(self_proj, ("wide", "narrow"), axis=1, tiled=True),
         lax.all_gather(norm_gains, ("wide", "narrow"), axis=1, tiled=True),
-        lax.all_gather(rel_table, ("wide", "narrow"), axis=0, tiled=True),
+        doubled_up(rel_table, ("wide", "narrow"), 0),
     )
     norm_scale = gains_full.astype(jnp.float32)
     select = jnp.asarray(bucket_select(length, table_full.shape[0]))

time: 798 us -> 773 us (0.969)
  blocking collectives: 209 us -> 171 us
  waiting for transfers between devices: 343 us -> 353 us
    all_gather x1 -> x0, blocking collectives: 37.8 us -> none  [body(): lax.all_gather(rel_table, ('wide', 'narrow'), axis=0, tiled=True)]
    unnamed x237 -> x239, local copies, waits for them, and re-layouts: 18.4 us -> 17.4 us
  transfers between devices with their start and end apart: 6 -> 11, of which waited for: 2 -> 6; matrix products, arithmetic and copies ran while one was open for 21% -> 22% of each run, Pallas kernels for 0% -> 0%
where the time goes in v1:
time: 773 us; the launch traced here: 768 us
  waiting for transfers between devices  353 us (46%)
  blocking collectives  171 us (22%)
  matrix products  90.6 us (12%)
  local copies, waits for them, and re-layouts  76.9 us (10%)
  other arithmetic  53.5 us (7%)
  between operations  16.9 us (2%)
    reduce_scatter x1, waiting for transfers between devices, body(): lax.psum_scatter(jnp.stack([grad_in, grad_out], axis=1), ('wide', 'narrow...  211 us
    reduce_scatter x1, waiting for transfers between devices, body(): lax.psum_scatter(jnp.stack([weight_grad(normed_two, grad_cross_query), we...  128 us
    psum x1, blocking collectives, body(): lax.psum((jnp.stack([scale_part, bias_part]), jnp.stack([self_head, cross...  46.5 us
    unnamed x1, blocking collectives  41.8 us
    all_gather x1, blocking collectives, body(): lax.all_gather(norm_gains, ('wide', 'narrow'), axis=1, tiled=True)  41.6 us
    psum x1, blocking collectives, body(): lax.psum((jnp.sum(memory_values, axis=(0, 1)), jnp.sum(memory_values * me...  40.6 us
    dot_general x9, matrix products, product(): return jnp.dot(left_side, right_side, preferred_element_type=jnp.float32)  24 us
    dot_general x8, matrix products, back_product(): jnp.einsum('ble,de->bld', upstream, weight, preferred_element_type=jnp.fl...  18.3 us
  transfers between devices with their start and end apart: 11, of which 6 were waited for; matrix products, arithmetic and copies ran while one was open for 22% of the time, Pallas kernels for 0%

profile of v1, /device:TPU:0, one launch (start us, length us, event | category | flops | bytes accessed | tf_op | source)
XLA Modules:
  0.0 768.1 jit_solution(6523100849593663572)
XLA Ops:
  13.9 41.8 %all-reduce.8 = (bf16[768]{0:T(1024)(128)(2,1)S(1)}, bf16[768]{0:T(1024)(128)(2,1)S(1)}, bf16[3072]{0:T(1024)(128)(2,1)S(1)}) all-reduce(bf16[768]{0:T(1024)(128)(2,1)S(1)} %dynamic-update-slice.1, bf16[768]{0:T(1024)(128)(2,1)S(1)} %dynamic-update-slice, ...), channel_id=1, replica_groups=mesh['wide'=16,'narrow'=2] {'wide','narrow'}, use_global_device_ids=true, to_apply=%add.4 | all-reduce | flops 4608 | bytes 18432
  55.7 1.7 convert_reduce_fusion
  57.4 40.6 %all-reduce.7 = (f32[768]{0:T(1024)S(1)}, f32[768]{0:T(1024)S(1)}) all-reduce(f32[768]{0:T(1024)S(1)} %get-tuple-element.19, f32[768]{0:T(1024)S(1)} %get-tuple-element.18), channel_id=1, replica_groups=mesh['wide'=16,'narrow'=2] {'wide','narrow'}, use_global_device_ids=true, to_apply=%region_9.10 | all-reduce | flops 1536 | bytes 12288 | tf_op jit(solution)/shard_map/psum | solution.py:194
  101.7 2.3 collective-permute-start.1
  105.7 2.1 collective-permute-start.2
  107.8 1.7 collective-permute-done.2
  110.4 41.6 %all-gather = bf16[32,24,5]{1,2,0:T(8,128)(2,1)S(1)} all-gather(bf16[1,24,5]{1,2,0:T(8,128)(2,1)S(1)} %bitcast.378), channel_id=1, replica_groups=mesh['wide'=16,'narrow'=2] {'wide','narrow'}, dimensions={0}, use_global_device_ids=true | all-gather | bytes 7920 | tf_op jit(solution)/shard_map/all_gather | solution.py:167
  154.9 4.8 collective-permute-done.4
  160.3 2.9 tile.4
  163.2 7.0 tile.10
  170.2 5.3 slice.107
  175.5 7.2 reshape.929
  182.7 2.8 slice.108
  185.4 2.3 copy.99
  187.8 1.8 convolution_convert_fusion.6
  189.7 1.9 convolution_convert_fusion.5
  192.5 1.8 convolution_convert_fusion.7
  194.5 2.6 fusion.109
  199.2 2.0 fusion.110
  202.7 2.5 convolution_convert_fusion.4
  205.1 1.9 copy.82
  207.1 3.3 convolution_convert_fusion.1
  210.4 1.6 multiply_reduce_fusion.1
  212.0 1.8 exponential_reduce_fusion
  214.4 1.5 convolution_convert_fusion.2
  215.9 3.0 multiply_convert_fusion.6
  221.7 4.5 all-gather.9.cloned.1.call-done
  226.2 8.8 %fusion.105 = (f32[200]{0:T(256)S(1)}, f32[200,3072]{1,0:T(8,128)S(1)}, f32[200,3072]{1,0:T(8,128)S(1)}, f32[200,3072]{1,0:T(8,128)S(1)}) fusion(bf16[2,768,3072]{2,1,0:T(8,128)(2,1)} %all-gather.9.cloned.1.call-done, f32[1,200,768]{2,1,0:T(8,128)} %copy-done.19, f32[768]{0:T(1024)S(1)} %copy-done.63, f32[200]{0:T(256)S(1)} %fusion.74, ...), kind=kOutput, calls=%fused_computation.242 | convolution fusion | flops 984268608 | bytes 12711264 | tf_op jit(solution)/shard_map/dot_general | solution.py:68
  236.5 1.6 multiply_reduce_fusion.2
  238.1 2.0 add_convert_fusion
  240.1 2.4 fusion.49
  244.4 2.1 fusion.35
  246.5 3.7 multiply_reduce_fusion
  250.2 2.3 multiply_convert_fusion
  252.5 1.6 fusion.24
  254.5 2.7 fusion.51
  259.0 1.8 fusion.31
  267.8 4.0 pad_maximum_fusion.1
  274.5 3.6 multiply_convert_fusion.1
  278.2 6.3 convolution_convert_fusion
  284.5 1.6 convolution_bitcast_fusion.3
  286.1 1.6 convolution_bitcast_fusion.4
  287.7 4.0 pad_maximum_fusion.2
  292.1 3.4 convolution_bitcast_fusion.1
  295.5 1.6 convolution_bitcast_fusion
  297.1 7.3 pad_maximum_fusion
  304.4 2.5 copy.100
  312.0 2.0 fusion.30
  314.1 1.8 convolution_add_fusion.2
  316.0 2.0 fusion.48
  320.4 2.2 pad.9.clone
  322.6 6.9 reshape.949
  329.6 3.1 fusion.34
  332.7 2.7 fusion.112
  338.2 2.5 pad_convert_fusion
  340.8 8.0 %reshape.955 = f32[12,200,400]{2,1,0:T(8,128)} reshape(f32[12,80000]{1,0:T(8,128)} %pad_convert_fusion) | data formatting | bytes 7680000 | tf_op jit(solution)/shard_map/transpose(jvp())/reshape | solution.py:51
  348.8 3.7 reduce_sum.426
  358.1 1.7 multiply_reduce_fusion.7
  361.1 46.5 %all-reduce.6 = (f32[2,768]{1,0:T(2,128)S(1)}, f32[3072]{0:T(1024)S(1)}, f32[5,768]{1,0:T(8,128)S(1)}, f32[512,12]{1,0:T(8,128)}, f32[2,12]{1,0:T(2,128)}) all-reduce(f32[2,768]{1,0:T(2,128)S(1)} %pad_maximum_fusion.8, f32[3072]{0:T(1024)} %get-tuple-element.12, ...), channel_id=1, replica_groups=mesh['wide'=16,'narrow'=2] {'wide','narrow'}, use_global_device_ids=true, to_apply=%region_36.37 | all-reduce | flops 14616 | bytes 116928 | tf_op jit(solution)/shard_map/psum | solution.py:339
  410.9 2.2 add_add_fusion.6
  413.1 4.0 fusion.13
  417.1 5.0 fusion.29
  422.1 127.9 %reduce-scatter.6.cloned.1.call-done = f32[24,4,768]{2,0,1:T(8,128)} async-done(((f32[768,4,768]{2,0,1:T(8,128)}), f32[24,4,768]{2,0,1:T(8,128)}) %reduce-scatter.6.cloned.1.call-update) | async-done | bytes 294928 | tf_op jit(solution)/shard_map/reduce_scatter | solution.py:274
  550.0 210.8 %reduce-scatter.8.cloned.1.call-done = f32[24,2,3072]{2,0,1:T(8,128)} async-done(((f32[768,2,3072]{2,0,1:T(8,128)}), f32[24,2,3072]{2,0,1:T(8,128)}) %reduce-scatter.8.cloned.1.call-update) | async-done | bytes 589840 | tf_op jit(solution)/shard_map/reduce_scatter | solution.py:242
  (361 shorter events, 59.1 us)
Async XLA Ops:
  7.2 152.6 %copy-start.47 = (f32[512,200]{1,0:T(8,128)S(1)}, f32[512,200]{1,0:T(8,128)}, u32[]{:S(2)}) copy-start(f32[512,200]{1,0:T(8,128)} %constant.148.clone) | copy-start | bytes 1228804
  7.2 96.9 %copy-start.4 = (bf16[1,200,768]{2,1,0:T(8,128)(2,1)S(1)}, bf16[1,200,768]{2,1,0:T(8,128)(2,1)}, u32[]{:S(2)}) copy-start(bf16[1,200,768]{2,1,0:T(8,128)(2,1)} %param.14) | copy-start | bytes 921604
  7.2 103.2 %copy-start.107 = (bf16[5,24]{1,0:T(8,128)(2,1)S(1)}, bf16[5,24]{1,0:T(8,128)(2,1)}, u32[]{:S(2)}) copy-start(bf16[5,24]{1,0:T(8,128)(2,1)} %param.22) | copy-start | bytes 724
  7.2 180.5 %all-gather.5.cloned.1.call-start = ((), (), s32[]{:S(2)}) async-start(), calls=%async_computation.3 | async-start | bytes 4866048 | tf_op jit(solution)/shard_map/all_gather | solution.py:166
  7.9 194.7 %all-gather.7.cloned.1.call-start = ((), (), s32[]{:S(2)}) async-start(), calls=%async_computation.4 | async-start | bytes 4866048 | tf_op jit(solution)/shard_map/all_gather | solution.py:189
  8.7 217.5 %all-gather.9.cloned.1.call-start = ((), (), s32[]{:S(2)}) async-start(), calls=%async_computation.5 | async-start | bytes 9732096 | tf_op jit(solution)/shard_map/all_gather | solution.py:214
  9.4 412.7 %reduce-scatter.4.cloned.1.call-start = ((), (), s32[]{:S(2)}) async-start(), calls=%async_computation.6 | async-start | bytes 9732096 | tf_op jit(solution)/shard_map/reduce_scatter | solution.py:321
  9.5 91.5 %collective-permute-start = (bf16[1,16,12]{2,1,0:T(8,128)(2,1)}, bf16[1,16,12]{2,1,0:T(8,128)(2,1)S(1)}, u32[]{:S(2)}, u32[]{:S(2)}) collective-permute-start(bf16[1,16,12]{2,1,0:T(8,128)(2,1)} %bitcast.373), channel_id=1, source_target_pairs={{0,1},{1,0},{2,3},{3,2},{4,5},{5,4},{6,7},{7,6},{8,9},{9,8},{10,11... | collective-permute-start | bytes 1160 | tf_op jit(solution)/shard_map/ppermute | solution.py:25
  99.7 92.8 %copy-start.67 = (f32[200]{0:T(256)}, f32[200]{0:T(256)S(1)}, u32[]{:S(2)}) copy-start(f32[200]{0:T(256)S(1)} %broadcast_multiply_fusion.6) | copy-start | bytes 2404
  101.7 4.0 collective-permute-start.1
  104.3 47.8 %copy-start.95 = (f32[200]{0:T(256)}, f32[200]{0:T(256)S(1)}, u32[]{:S(2)}) copy-start(f32[200]{0:T(256)S(1)} %fusion.47) | copy-start | bytes 2404
  105.7 3.8 collective-permute-start.2
  107.8 84.7 %copy-start.71 = (f32[200]{0:T(256)}, f32[200]{0:T(256)S(1)}, u32[]{:S(2)}) copy-start(f32[200]{0:T(256)S(1)} %fusion.70) | copy-start | bytes 2404
  109.6 42.8 %collective-permute-start.3 = (bf16[8,16,12]{2,1,0:T(8,128)(2,1)S(1)}, bf16[8,16,12]{2,1,0:T(8,128)(2,1)S(1)}, u32[]{:S(2)}, u32[]{:S(2)}) collective-permute-start(bf16[8,16,12]{2,1,0:T(8,128)(2,1)S(1)} %bitcast.362), channel_id=1, source_target_pairs={{0,8},{1,9},{2,10},{3,11},{4,12},{5,13},{6,14},{7,15},{8,0},{9,1},... | collective-permute-start | bytes 9224 | tf_op jit(solution)/shard_map/ppermute | solution.py:25
  152.4 7.3 collective-permute-start.4
  189.7 4.8 copy-start.44
  202.1 5.0 copy-start.76
  202.1 5.0 copy-start.80
  202.1 5.0 copy-start.102
  202.1 5.0 copy-start.104
  207.1 6.8 slice-start.3
  212.0 3.9 copy-start
  214.4 35.8 %copy-start.58 = (f32[12,200]{1,0:T(8,128)}, f32[12,200]{1,0:T(8,128)S(1)}, u32[]{:S(2)}) copy-start(f32[12,200]{1,0:T(8,128)S(1)} %log_add_fusion) | copy-start | bytes 28804
  219.0 7.2 copy-start.63
  220.6 22.0 %copy-start.84 = (f32[200]{0:T(256)}, f32[200]{0:T(256)S(1)}, u32[]{:S(2)}) copy-start(f32[200]{0:T(256)S(1)} %broadcast_multiply_fusion.2) | copy-start | bytes 2404
  221.6 20.9 %copy-start.91 = (f32[200]{0:T(256)}, f32[200]{0:T(256)S(1)}, u32[]{:S(2)}) copy-start(f32[200]{0:T(256)S(1)} %fusion.74) | copy-start | bytes 2404
  226.2 8.8 %copy-start.32 = (bf16[1,200,768]{2,1,0:T(8,128)(2,1)S(1)}, bf16[1,200,768]{2,1,0:T(8,128)(2,1)}, u32[]{:S(2)}) copy-start(bf16[1,200,768]{2,1,0:T(8,128)(2,1)} %param.17) | copy-start | bytes 921604
  226.2 8.9 %copy-start.60 = (f32[3072]{0:T(1024)S(1)}, f32[3072]{0:T(1024)}, u32[]{:S(2)}) copy-start(f32[3072]{0:T(1024)} %convert_element_type.192) | copy-start | bytes 36868
  226.2 8.9 %copy-start.108 = (bf16[2,768,3072]{2,1,0:T(8,128)(2,1)S(1)}, bf16[2,768,3072]{2,1,0:T(8,128)(2,1)}, u32[]{:S(2)}) copy-start(bf16[2,768,3072]{2,1,0:T(8,128)(2,1)} %all-gather.9.cloned.1.call-done) | copy-start | bytes 28311556
  240.1 6.3 slice-start
  240.1 6.3 slice-start.1
  242.6 3.9 slice-start.2
  244.4 5.8 copy-start.25
  246.4 3.8 copy-start.6
  262.1 3.7 copy-start.39
  271.8 278.2 %reduce-scatter.6.cloned.1.call-start = ((), (), s32[]{:S(2)}) async-start(), calls=%async_computation.7 | async-start | bytes 9732096 | tf_op jit(solution)/shard_map/reduce_scatter | solution.py:274
  274.5 3.6 copy-start.100
  278.1 8.0 %copy-start.55 = (bf16[12,64,896]{2,1,0:T(8,128)(2,1)}, bf16[12,64,896]{2,1,0:T(8,128)(2,1)S(1)}, u32[]{:S(2)}) copy-start(bf16[12,64,896]{2,1,0:T(8,128)(2,1)S(1)} %multiply_convert_fusion.1) | copy-start | bytes 4128772
  278.1 6.3 copy-start.10
  278.2 6.3 copy-start.77
  278.2 6.3 copy-start.81
  278.2 6.3 copy-start.103
  278.2 6.3 copy-start.105
  291.8 3.7 copy-start.3
  291.8 469.1 %reduce-scatter.8.cloned.1.call-start = ((), (), s32[]{:S(2)}) async-start(), calls=%async_computation.8 | async-start | bytes 19464192 | tf_op jit(solution)/shard_map/reduce_scatter | solution.py:242
  306.9 7.2 copy-start.42
  312.0 3.9 copy-start.40
  312.0 3.9 copy-start.69
  314.1 3.9 copy-start.96
  314.1 4.8 copy-start.73
  315.9 4.5 copy-start.31
  358.0 52.8 %copy-start.106 = (f32[200]{0:T(256)S(1)}, f32[200]{0:T(256)}, u32[]{:S(2)}) copy-start(f32[200]{0:T(256)} %get-tuple-element.27) | copy-start | bytes 2404
  358.0 52.8 %copy-start.23 = (f32[1,200,768]{2,1,0:T(8,128)S(1)}, f32[1,200,768]{2,1,0:T(8,128)}, u32[]{:S(2)}) copy-start(f32[1,200,768]{2,1,0:T(8,128)} %copy-done.22) | copy-start | bytes 1843204
  358.0 52.8 %copy-start.70 = (f32[200]{0:T(256)S(1)}, f32[200]{0:T(256)}, u32[]{:S(2)}) copy-start(f32[200]{0:T(256)} %copy-done.67) | copy-start | bytes 2404
  358.0 52.8 %copy-start.74 = (f32[200]{0:T(256)S(1)}, f32[200]{0:T(256)}, u32[]{:S(2)}) copy-start(f32[200]{0:T(256)} %copy-done.71) | copy-start | bytes 2404
  358.0 52.8 %copy-start.98 = (f32[200]{0:T(256)S(1)}, f32[200]{0:T(256)}, u32[]{:S(2)}) copy-start(f32[200]{0:T(256)} %copy-done.97) | copy-start | bytes 2404
  358.0 55.0 %copy-start.79 = (f32[768]{0:T(1024)S(1)}, f32[768]{0:T(1024)}, u32[]{:S(2)}) copy-start(f32[768]{0:T(1024)} %get-tuple-element.62) | copy-start | bytes 9220
  358.0 55.0 %copy-start.83 = (f32[768]{0:T(1024)S(1)}, f32[768]{0:T(1024)}, u32[]{:S(2)}) copy-start(f32[768]{0:T(1024)} %get-tuple-element.67) | copy-start | bytes 9220
  358.1 55.0 %copy-start.92 = (f32[768]{0:T(1024)S(1)}, f32[768]{0:T(1024)}, u32[]{:S(2)}) copy-start(f32[768]{0:T(1024)} %get-tuple-element.61) | copy-start | bytes 9220
  407.7 5.4 copy-start.12
  413.1 4.0 copy-start.21
  413.1 4.0 copy-start.62
  413.1 4.0 copy-start.87
  413.1 4.0 copy-start.90
  (61 other events, 140.8 us)
Sparse Core Ops, SparseCore 0:
  11.0 66.9 all-gather.4
  80.9 62.2 all-gather.6
  146.2 79.9 all-gather.8
  272.0 136.5 reduce-scatter.3
  414.9 135.1 reduce-scatter.5
  556.9 203.9 reduce-scatter.7
